TPU v7x, 32 devices: a whole 2x2x4 slice. The times are simulated.
32 devices in a mesh: grp: 8 (over z, y), col: 4 (over x, core).
Axes of the slice: x: 2, y: 2, z: 4, core: 2. Of those that a mesh axis runs over, the one named last changes fastest.
Arguments:
- features: bfloat16 [65536, 256], P(('grp', 'col')), may hold values from -6 to 6
- adj_tiles: bfloat16 [1536, 256, 256], P('grp'), may hold values from 0 to 1.5
- block_pairs: int32 [8, 192, 2], P('grp'), may hold values from 0 to 31, as said below
- tile_count: int32 [8], P('grp'), may hold values from 32 to 192, as said below
- degree: int32 [65536], P('grp'), may hold values from 1 to 769
- labels: int32 [65536], P(('grp', 'col')), may hold values from 0 to 63
- loss_mask: int32 [65536], P(('grp', 'col')), may hold values from 0 to 1
- slot_piece: int32 [8, 79], replicated, may hold values from -1 to 416, as said below
- master: float32 [632, 2, 256], P('grp', None, 'col'), may hold values from -4 to 4
- moment_one: float32 [632, 2, 256], P('grp', None, 'col'), may hold values from -0.125 to 0.125
- moment_two: float32 [632, 2, 256], P('grp', None, 'col'), may hold values from 3.0517579e-06 to 0.00030517578
Outputs:
- mean_loss: float32 [], replicated
- new_master: float32 [632, 2, 256], P('grp', None, 'col')
- new_moment_one: float32 [632, 2, 256], P('grp', None, 'col')
- new_moment_two: float32 [632, 2, 256], P('grp', None, 'col')
- new_weights: bfloat16 [632, 2, 256], P('grp', None, 'col')
Inputs may be any that keep to these rules, and one draw needn't show every extreme that they name: `block_pairs`: of each group, the first tile_count entries are distinct pairs of blocks and include every diagonal pair (r, r); later entries are padding. `tile_count`: some group has 192 live tiles in every draw. `slot_piece`: each piece 0 to 416 sits in exactly one slot; a group holds at most 79 pieces, and some group holds 79 in every draw.
All inputs are finite; a program needn't handle non-finite values.
Results may differ from a plain program's by a relative error of at most 0.0079.
Values may be sent and summed in bfloat16 or wider, within the bound.
A program may use at most 128 MiB of HBM per device.

v0:
```python
import jax
import jax.numpy as jnp
from jax import lax
from jax.sharding import PartitionSpec as P

F = 256
HID = 256
CLS = 64
B = 256
PR = 2
STEP = 7
PROWS = 834
PIECES = 417
learn_rate = 0.01
beta_one = 0.5
beta_two = 0.5
adam_epsilon = 1e-08
decay_rate = 0.1


def contract_rows(left, right):
    return lax.dot_general(
        left, right, (((0,), (0,)), ((), ())), preferred_element_type=jnp.float32
    )


def contract_cols(left, right):
    return lax.dot_general(
        left, right, (((1,), (1,)), ((), ())), preferred_element_type=jnp.float32
    )


def body(
    features,
    adj_tiles,
    block_pairs,
    tile_count,
    degree,
    labels,
    loss_mask,
    slot_piece,
    master,
    moment_one,
    moment_two,
):
    col_count = lax.axis_size("col")
    grp_count = lax.axis_size("grp")
    col_index = lax.axis_index("col")
    grp_index = lax.axis_index("grp")
    node_rows = features.shape[0]
    group_nodes = degree.shape[0]
    block_count = group_nodes // B
    tile_slots = adj_tiles.shape[0]
    slot_width = slot_piece.shape[1]
    col_width = master.shape[2]
    own_slots = master.astype(jnp.bfloat16)[None]
    gathered = lax.all_gather(own_slots, ("grp", "col"), axis=0, tiled=True)
    slot_values = gathered.reshape(grp_count, col_count, slot_width, PR, col_width)
    slot_values = slot_values.transpose(0, 2, 3, 1, 4).reshape(
        grp_count * slot_width, PR, col_count * col_width
    )
    flat_slots = slot_piece.reshape(-1)
    positions = jnp.arange(flat_slots.shape[0], dtype=jnp.int32)
    target = jnp.where(flat_slots >= 0, flat_slots, PIECES)
    piece_slot = jnp.zeros((PIECES + 1,), jnp.int32).at[target].set(positions)[:PIECES]
    weight_table = slot_values[piece_slot].reshape(PROWS, HID)
    encoder_weight = weight_table[:F]
    self_weight = weight_table[F : F + HID]
    neigh_weight = weight_table[F + HID : F + 2 * HID]
    head_weight = weight_table[F + 2 * HID : F + 2 * HID + CLS]
    encoder_bias = weight_table[PROWS - 2].astype(jnp.float32)
    sage_bias = weight_table[PROWS - 1].astype(jnp.float32)
    mask_values = loss_mask.astype(jnp.float32)
    labelled = lax.psum(jnp.sum(mask_values), ("grp", "col"))
    preact = jnp.dot(features, encoder_weight, preferred_element_type=jnp.float32) + encoder_bias
    sig_pre = jax.nn.sigmoid(preact)
    encoded = (preact * sig_pre).astype(jnp.bfloat16)
    enc_columns = lax.all_to_all(encoded, "col", split_axis=1, concat_axis=0, tiled=True)
    pairs = block_pairs[0]
    row_blocks = pairs[:, 0]
    col_blocks = pairs[:, 1]
    live_tiles = jnp.arange(tile_slots, dtype=jnp.int32) < tile_count[0]
    block_ids = jnp.arange(block_count, dtype=jnp.int32)
    row_places = ((row_blocks[None, :] == block_ids[:, None]) & live_tiles[None, :]).astype(
        jnp.float32
    )
    picked = enc_columns.reshape(block_count, B, -1)[col_blocks]
    products = jnp.einsum("tij,tjc->tic", adj_tiles, picked, preferred_element_type=jnp.float32)
    block_sums = jnp.einsum("rt,tic->ric", row_places, products, precision=lax.Precision.HIGHEST)
    degree_values = degree.astype(jnp.float32)
    mean_columns = (block_sums.reshape(group_nodes, -1) / degree_values[:, None]).astype(
        jnp.bfloat16
    )
    neigh_mean = lax.all_to_all(mean_columns, "col", split_axis=0, concat_axis=1, tiled=True)
    sage_pre = (
        jnp.dot(encoded, self_weight, preferred_element_type=jnp.float32)
        + jnp.dot(neigh_mean, neigh_weight, preferred_element_type=jnp.float32)
        + sage_bias
    )
    sig_sage = jax.nn.sigmoid(sage_pre)
    hidden = (sage_pre * sig_sage).astype(jnp.bfloat16)
    logits = contract_cols(hidden, head_weight)
    row_max = jnp.max(logits, axis=1, keepdims=True)
    log_total = row_max[:, 0] + jnp.log(jnp.sum(jnp.exp(logits - row_max), axis=1))
    label_hot = (labels[:, None] == jnp.arange(CLS, dtype=jnp.int32)[None, :]).astype(jnp.float32)
    target_logit = jnp.sum(logits * label_hot, axis=1)
    local_loss = jnp.sum(mask_values * (log_total - target_logit))
    probability = jnp.exp(logits - log_total[:, None])
    logit_grad = ((probability - label_hot) * mask_values[:, None] / labelled).astype(jnp.bfloat16)
    head_grad = contract_rows(logit_grad, hidden)
    hidden_grad = jnp.dot(logit_grad, head_weight, preferred_element_type=jnp.float32)
    sage_grad = (hidden_grad * sig_sage * (1.0 + sage_pre * (1.0 - sig_sage))).astype(jnp.bfloat16)
    self_grad = contract_rows(encoded, sage_grad)
    neigh_grad = contract_rows(neigh_mean, sage_grad)
    sage_bias_grad = jnp.sum(sage_grad.astype(jnp.float32), axis=0)
    self_back = contract_cols(sage_grad, self_weight)
    neigh_back = contract_cols(sage_grad, neigh_weight)
    degree_rows = lax.dynamic_slice_in_dim(degree_values, col_index * node_rows, node_rows)
    sum_grad = (neigh_back / degree_rows[:, None]).astype(jnp.bfloat16)
    grad_columns = lax.all_to_all(sum_grad, "col", split_axis=1, concat_axis=0, tiled=True)
    picked_grad = grad_columns.reshape(block_count, B, -1)[row_blocks]
    back_products = jnp.einsum(
        "tij,tic->tjc", adj_tiles, picked_grad, preferred_element_type=jnp.float32
    )
    col_places = ((col_blocks[None, :] == block_ids[:, None]) & live_tiles[None, :]).astype(
        jnp.float32
    )
    back_blocks = jnp.einsum(
        "rt,tjc->rjc", col_places, back_products, precision=lax.Precision.HIGHEST
    )
    neigh_return = lax.all_to_all(
        back_blocks.reshape(group_nodes, -1).astype(jnp.bfloat16),
        "col",
        split_axis=0,
        concat_axis=1,
        tiled=True,
    ).astype(jnp.float32)
    encoded_grad = self_back + neigh_return
    preact_grad = (encoded_grad * sig_pre * (1.0 + preact * (1.0 - sig_pre))).astype(jnp.bfloat16)
    encoder_grad = contract_rows(features, preact_grad)
    encoder_bias_grad = jnp.sum(preact_grad.astype(jnp.float32), axis=0)
    grad_table = jnp.concatenate(
        [
            encoder_grad,
            self_grad,
            neigh_grad,
            head_grad,
            encoder_bias_grad[None, :],
            sage_bias_grad[None, :],
        ],
        axis=0,
    )
    loss_total = lax.psum(local_loss, ("grp", "col"))
    mean_loss = loss_total / labelled
    group_grad = lax.psum_scatter(
        grad_table.astype(jnp.bfloat16), "col", scatter_dimension=1, tiled=True
    ).astype(jnp.float32)
    my_pieces = lax.dynamic_slice_in_dim(slot_piece, grp_index, 1, 0)[0]
    is_owned = my_pieces >= 0
    safe_pieces = jnp.where(is_owned, my_pieces, 0)
    owned_values = is_owned[:, None, None]
    total_grad = lax.psum(group_grad, "grp")
    slot_grad = jnp.where(owned_values, total_grad.reshape(PIECES, PR, -1)[safe_pieces], 0.0)
    table_rows = safe_pieces[:, None] * PR + jnp.arange(PR, dtype=jnp.int32)[None, :]
    decay_values = jnp.where(table_rows < PROWS - 2, decay_rate, 0.0)[:, :, None]
    first_moment = beta_one * moment_one + (1.0 - beta_one) * slot_grad
    second_moment = beta_two * moment_two + (1.0 - beta_two) * slot_grad * slot_grad
    first_hat = first_moment / (1.0 - beta_one**STEP)
    second_hat = second_moment / (1.0 - beta_two**STEP)
    updated = master - learn_rate * (
        first_hat / (jnp.sqrt(second_hat) + adam_epsilon) + decay_values * master
    )
    updated = jnp.where(owned_values, updated, 0.0)
    first_moment = jnp.where(owned_values, first_moment, 0.0)
    second_moment = jnp.where(owned_values, second_moment, 0.0)
    return (mean_loss, updated, first_moment, second_moment, updated.astype(jnp.bfloat16))


def solution(mesh):
    in_specs = (
        P(("grp", "col"), None),
        P("grp", None, None),
        P("grp", None, None),
        P("grp"),
        P("grp"),
        P(("grp", "col")),
        P(("grp", "col")),
        P(),
        P("grp", None, "col"),
        P("grp", None, "col"),
        P("grp", None, "col"),
    )
    out_specs = (
        P(),
        P("grp", None, "col"),
        P("grp", None, "col"),
        P("grp", None, "col"),
        P("grp", None, "col"),
    )
    return jax.shard_map(body, mesh=mesh, in_specs=in_specs, out_specs=out_specs, check_vma=False)
```

profile of v0, /device:TPU:0, one launch (start us, length us, event | category | flops | bytes accessed | tf_op | source)
XLA Modules:
  0.0 409.3 jit_solution(9063719519104682953)
XLA Ops:
  8.2 46.8 %all-gather = bf16[2528,2,64]{2,1,0:T(2,128)(2,1)S(1)} all-gather(bf16[79,2,64]{2,1,0:T(2,128)(2,1)S(1)} %copy.83), channel_id=2, replica_groups=mesh['grp'=8,'col'=4] {'grp','col'}, dimensions={0}, use_global_device_ids=true | all-gather | bytes 667392 | tf_op jit(solution)/shard_map/all_gather | solution.py:57
  58.3 4.1 scatter_custom_fusion
  62.4 2.7 gather_fusion
  66.7 2.5 multiply_convert_fusion.1
  69.2 3.9 all-to-all-start
  73.9 13.6 %all-to-all-done = bf16[2048,4,64]{0,2,1:T(8,128)(2,1)S(1)} async-done(((bf16[2048,4,64]{0,2,1:T(8,128)(2,1)}), bf16[2048,4,64]{0,2,1:T(8,128)(2,1)S(1)}, u32[]{:S(2)}, u32[]{:S(2)}) %all-to-all-start) | async-done | bytes 1048608 | tf_op jit(solution)/shard_map/all_to_all | solution.py:78
  89.9 1.8 copy.87
  91.8 8.0 %gather_fusion.1 = bf16[192,256,64]{1,2,0:T(8,128)(2,1)} fusion(bf16[32,256,64]{1,2,0:T(8,128)(2,1)S(1)} %copy.87, s32[1024]{0:T(1024)S(1)} %pad_clamp_fusion.2), kind=kCustom, calls=%fused_computation.1 | custom fusion | bytes 12583680 | tf_op jit(solution)/shard_map/gather | solution.py:87
  99.7 18.3 %convolution_bitcast_fusion.1 = f32[192,256,64]{1,2,0:T(8,128)} fusion(bf16[192,256,64]{1,2,0:T(8,128)(2,1)} %gather_fusion.1, bf16[192,256,256]{2,1,0:T(8,128)(2,1)} %param.12), kind=kOutput, calls=%fused_computation.10 | convolution fusion | flops 1610612736 | bytes 44040192 | tf_op jit(solution)/shard_map/tij,tjc->tic/dot_general | solution.py:88
  118.1 16.9 %fusion.2 = f32[32,256,64]{1,0,2:T(8,128)} fusion(f32[192,256,64]{1,2,0:T(8,128)} %convolution_bitcast_fusion.1, s32[192]{0:T(256)S(1)} %bitcast.95, pred[192]{0:T(512)(128)(4,1)S(1)} %iota_compare_fusion.3), kind=kOutput, calls=%fused_computation.7 | convolution fusion | flops 1207971840 | bytes 14681024 | tf_op jit(solution)/shard_map/rt,tic->ric/dot_general | solution.py:89
  134.9 2.2 reshape.175
  137.1 2.1 fusion.12
  139.3 3.6 all-to-all-start.1
  143.1 3.0 fusion.40
  146.2 11.1 %all-to-all-done.1 = bf16[4,2048,64]{1,2,0:T(8,128)(2,1)S(1)} async-done(((bf16[4,2048,64]{1,2,0:T(8,128)(2,1)}), bf16[4,2048,64]{1,2,0:T(8,128)(2,1)S(1)}, u32[]{:S(2)}, u32[]{:S(2)}) %all-to-all-start.1) | async-done | bytes 1048608 | tf_op jit(solution)/shard_map/all_to_all | solution.py:94
  157.3 3.7 multiply_convert_fusion
  163.1 37.2 %all-reduce = (f32[]{:T(128)}, f32[]{:T(128)}) all-reduce(f32[]{:T(128)} %get-tuple-element.27, f32[]{:T(128)} %get-tuple-element.28), channel_id=1, replica_groups=mesh['grp'=8,'col'=4] {'grp','col'}, use_global_device_ids=true, to_apply=%region_7.8 | all-reduce | flops 2 | bytes 16 | tf_op jit(solution)/shard_map/psum | solution.py:74
  200.4 3.4 fusion.39
  205.2 3.5 all-to-all-start.2
  208.8 14.4 %all-to-all-done.2 = bf16[2048,4,64]{0,2,1:T(8,128)(2,1)S(1)} async-done(((bf16[2048,4,64]{0,2,1:T(8,128)(2,1)}), bf16[2048,4,64]{0,2,1:T(8,128)(2,1)S(1)}, u32[]{:S(2)}, u32[]{:S(2)}) %all-to-all-start.2) | async-done | bytes 1048608 | tf_op jit(solution)/shard_map/all_to_all | solution.py:120
  223.2 1.8 copy.94
  225.0 2.6 reshape.176
  227.6 1.8 copy.95
  229.4 8.0 %gather_fusion.2 = bf16[192,256,64]{1,2,0:T(8,128)(2,1)} fusion(bf16[32,256,64]{1,2,0:T(8,128)(2,1)S(1)} %copy.95, s32[1024]{0:T(1024)S(1)} %pad_clamp_fusion.1), kind=kCustom, calls=%fused_computation.2 | custom fusion | bytes 12583680 | tf_op jit(solution)/shard_map/gather | solution.py:121
  237.3 19.0 %convolution_bitcast_fusion = f32[192,256,64]{1,2,0:T(8,128)} fusion(bf16[192,256,64]{1,2,0:T(8,128)(2,1)} %gather_fusion.2, bf16[192,256,256]{2,1,0:T(8,128)(2,1)} %param.12), kind=kOutput, calls=%fused_computation.9 | convolution fusion | flops 1610612736 | bytes 44040192 | tf_op jit(solution)/shard_map/tij,tic->tjc/dot_general | solution.py:122
  256.3 16.4 %fusion.13 = bf16[32,256,64]{1,0,2:T(8,128)(2,1)} fusion(f32[192,256,64]{1,2,0:T(8,128)} %convolution_bitcast_fusion, s32[192]{0:T(256)S(1)} %bitcast.94, pred[192]{0:T(512)(128)(4,1)S(1)} %iota_compare_fusion.3), kind=kOutput, calls=%fused_computation.30 | convolution fusion | flops 1208496128 | bytes 13632448 | tf_op jit(solution)/shard_map/rt,tjc->rjc/dot_general | solution.py:128
  272.8 1.9 convert_element_type.80
  276.2 3.5 all-to-all-start.3
  279.8 3.2 convolution_convert_fusion.3
  285.1 9.0 %all-to-all-done.3 = bf16[4,2048,64]{1,2,0:T(8,128)(2,1)S(1)} async-done(((bf16[4,2048,64]{1,2,0:T(8,128)(2,1)}), bf16[4,2048,64]{1,2,0:T(8,128)(2,1)S(1)}, u32[]{:S(2)}, u32[]{:S(2)}) %all-to-all-start.3) | async-done | bytes 1048608 | tf_op jit(solution)/shard_map/all_to_all | solution.py:131
  299.1 21.4 %reduce-scatter.4.cloned.1.call-done = bf16[64,834]{1,0:T(8,128)(2,1)} async-done(((bf16[256,834]{1,0:T(8,128)(2,1)}), bf16[64,834]{1,0:T(8,128)(2,1)}) %reduce-scatter.4.cloned.1.call-update) | async-done | bytes 106768
  324.1 71.9 %all-reduce.3.cloned.1.call-done = f32[417,2,64]{2,1,0:T(2,128)} async-done(((f32[417,2,64]{2,1,0:T(2,128)}), f32[417,2,64]{2,1,0:T(2,128)}) %all-reduce.3.cloned.1.call-update) | async-done | bytes 213520 | tf_op jit(solution)/shard_map/psum | solution.py:162
  (102 shorter events, 27.9 us)
Async XLA Ops:
  7.2 59.5 %copy-start = (bf16[2048,256]{1,0:T(8,128)(2,1)S(1)}, bf16[2048,256]{1,0:T(8,128)(2,1)}, u32[]{:S(2)}) copy-start(bf16[2048,256]{1,0:T(8,128)(2,1)} %param.11) | copy-start | bytes 3145732
  55.0 3.2 copy-start.15
  65.1 4.1 %copy-start.4 = (bf16[417,2,256]{2,1,0:T(2,128)(2,1)}, bf16[417,2,256]{2,1,0:T(2,128)(2,1)S(1)}, u32[]{:S(2)}) copy-start(bf16[417,2,256]{2,1,0:T(2,128)(2,1)S(1)} %gather_fusion) | copy-start | bytes 1281028
  69.2 4.6 %copy-start.11 = (s32[8192]{0:T(1024)S(1)}, s32[8192]{0:T(1024)}, u32[]{:S(2)}) copy-start(s32[8192]{0:T(1024)} %param.15) | copy-start | bytes 98308
  69.2 4.7 %copy-start.16 = (s32[1,192,2]{1,2,0:T(2,128)S(1)}, s32[1,192,2]{1,2,0:T(2,128)}, u32[]{:S(2)}) copy-start(s32[1,192,2]{1,2,0:T(2,128)} %param.13) | copy-start | bytes 4612
  69.2 18.3 %all-to-all-start = ((bf16[2048,4,64]{0,2,1:T(8,128)(2,1)}), bf16[2048,4,64]{0,2,1:T(8,128)(2,1)S(1)}, u32[]{:S(2)}, u32[]{:S(2)}) async-start(bf16[2048,4,64]{0,2,1:T(8,128)(2,1)} %bitcast.8), calls=%async_computation | async-start | bytes 2097152 | tf_op jit(solution)/shard_map/all_to_all | solution.py:78
  73.9 13.7 %copy-start.8 = (f32[8192]{0:T(1024)}, f32[8192]{0:T(1024)S(1)}, u32[]{:S(2)}) copy-start(f32[8192]{0:T(1024)S(1)} %convert_element_type.72) | copy-start | bytes 98308
  139.2 3.8 slice-start
  139.2 3.8 copy-start.12
  139.3 18.1 %all-to-all-start.1 = ((bf16[4,2048,64]{1,2,0:T(8,128)(2,1)}), bf16[4,2048,64]{1,2,0:T(8,128)(2,1)S(1)}, u32[]{:S(2)}, u32[]{:S(2)}) async-start(bf16[4,2048,64]{1,2,0:T(8,128)(2,1)} %fusion.12), calls=%async_computation.1 | async-start | bytes 2097152 | tf_op jit(solution)/shard_map/all_to_all | solution.py:94
  142.9 14.4 %copy-start.17 = (f32[1,256]{1,0:T(1,128)S(1)}, f32[1,256]{1,0:T(1,128)}, u32[]{:S(2)}) copy-start(f32[1,256]{1,0:T(1,128)} %get-tuple-element.34) | copy-start | bytes 3076
  157.3 5.0 %copy-start.14 = (s32[2048]{0:T(1024)S(1)}, s32[2048]{0:T(1024)}, u32[]{:S(2)}) copy-start(s32[2048]{0:T(1024)} %param.16) | copy-start | bytes 24580
  161.0 1.0 copy-start.6
  162.3 41.4 %copy-start.5 = (f32[2048,64]{0,1:T(8,128)}, f32[2048,64]{0,1:T(8,128)S(1)}, u32[]{:S(2)}) copy-start(f32[2048,64]{0,1:T(8,128)S(1)} %get-tuple-element.50) | copy-start | bytes 1572868
  200.4 3.4 dynamic-slice-start
  203.8 1.5 copy-start.1
  205.2 18.0 %all-to-all-start.2 = ((bf16[2048,4,64]{0,2,1:T(8,128)(2,1)}), bf16[2048,4,64]{0,2,1:T(8,128)(2,1)S(1)}, u32[]{:S(2)}, u32[]{:S(2)}) async-start(bf16[2048,4,64]{0,2,1:T(8,128)(2,1)} %bitcast.92), calls=%async_computation.2 | async-start | bytes 2097152 | tf_op jit(solution)/shard_map/all_to_all | solution.py:120
  276.2 17.9 %all-to-all-start.3 = ((bf16[4,2048,64]{1,2,0:T(8,128)(2,1)}), bf16[4,2048,64]{1,2,0:T(8,128)(2,1)S(1)}, u32[]{:S(2)}, u32[]{:S(2)}) async-start(bf16[4,2048,64]{1,2,0:T(8,128)(2,1)} %copy.97), calls=%async_computation.3 | async-start | bytes 2097152 | tf_op jit(solution)/shard_map/all_to_all | solution.py:131
  279.7 40.9 %reduce-scatter.4.cloned.1.call-start = ((), (), s32[]{:S(2)}) async-start(), calls=%async_computation.6 | async-start | bytes 573440
  279.7 3.2 copy-start.2
  285.1 9.2 %copy-start.3 = (bf16[2048,256]{0,1:T(8,128)(2,1)S(1)}, bf16[2048,256]{0,1:T(8,128)(2,1)}, u32[]{:S(2)}) copy-start(bf16[2048,256]{0,1:T(8,128)(2,1)} %copy-done.1) | copy-start | bytes 3145732
  294.1 1.6 copy-start.18
  296.9 0.8 copy-start.13
  296.9 1.9 copy-start.7
  296.9 2.0 copy-start.9
  296.9 2.1 copy-start.10
  298.7 97.4 %all-reduce.3.cloned.1.call-start = ((), (), s32[]{:S(2)}) async-start(), calls=%async_computation.5 | async-start | bytes 854016 | tf_op jit(solution)/shard_map/psum | solution.py:162
Sparse Core Ops, SparseCore 0:
  298.8 21.7 reduce-scatter.3
  324.0 72.0 all-reduce.2
where the time goes:
time: 415 us; the launch traced here: 409 us
  waiting for transfers between devices  142 us (34%)
  matrix products  92.1 us (22%)
  blocking collectives  84 us (20%)
  local copies, waits for them, and re-layouts  53.8 us (13%)
  between operations  17.9 us (4%)
  starting transfers between devices  14.7 us (4%)
  other arithmetic  5.23 us (1%)
    psum x1, waiting for transfers between devices, body(): total_grad = lax.psum(group_grad, 'grp')  71.9 us
    all_gather x1, blocking collectives, body(): gathered = lax.all_gather(own_slots, ('grp', 'col'), axis=0, tiled=True)  46.8 us
    psum x1, blocking collectives, body(): labelled = lax.psum(jnp.sum(mask_values), ('grp', 'col'))  37.2 us
    unnamed x3, waiting for transfers between devices  21.5 us
    dot_general x1, matrix products, body(): jnp.einsum('tij,tic->tjc', adj_tiles, picked_grad, preferred_element_type...  19 us
    dot_general x1, matrix products, body(): jnp.einsum('tij,tjc->tic', adj_tiles, picked, preferred_element_type=jnp....  18.3 us
    dot_general x1, matrix products, body(): jnp.einsum('rt,tic->ric', row_places, products, precision=lax.Precision.H...  16.9 us
    dot_general x1, matrix products, body(): jnp.einsum('rt,tjc->rjc', col_places, back_products, precision=lax.Precis...  16.4 us
  transfers between devices with their start and end apart: 6, of which 6 were waited for; matrix products, arithmetic and copies ran while one was open for 2% of the time, Pallas kernels for 0%

commit v1 on v0

--- a/solution.py
+++ b/solution.py
@@ -159,7 +159,10 @@
     is_owned = my_pieces >= 0
     safe_pieces = jnp.where(is_owned, my_pieces, 0)
     owned_values = is_owned[:, None, None]
-    total_grad = lax.psum(group_grad, "grp")
+    size, total_grad = (lax.axis_size("grp"), group_grad)
+    for far in [1 << k for k in range(size.bit_length() - 1)]:
+        swap = [(i, i ^ far) for i in range(size)]
+        total_grad = total_grad + lax.ppermute(total_grad, "grp", swap)
     slot_grad = jnp.where(owned_values, total_grad.reshape(PIECES, PR, -1)[safe_pieces], 0.0)
     table_rows = safe_pieces[:, None] * PR + jnp.arange(PR, dtype=jnp.int32)[None, :]
     decay_values = jnp.where(table_rows < PROWS - 2, decay_rate, 0.0)[:, :, None]

time: 415 us -> 383 us (0.923)
  waiting for transfers between devices: 142 us -> 105 us
  starting transfers between devices: 14.7 us -> 20.5 us
    psum x1 -> x0, waiting for transfers between devices: 71.9 us -> none  [body(): total_grad = lax.psum(group_grad, 'grp')]
    ppermute x0 -> x3, waiting for transfers between devices: none -> 35.2 us  [body(): total_grad = total_grad + lax.ppermute(total_grad, 'grp', swap)]
    ppermute x0 -> x3, starting transfers between devices: none -> 5.54 us  [body(): total_grad = total_grad + lax.ppermute(total_grad, 'grp', swap)]
    unnamed x3 -> x2, waiting for transfers between devices: 21.5 us -> 21.6 us
  transfers between devices with their start and end apart: 6 -> 8, of which waited for: 6 -> 8; matrix products, arithmetic and copies ran while one was open for 2% -> 2% of each run, Pallas kernels for 0% -> 0%
where the time goes in v1:
time: 383 us; the launch traced here: 377 us
  waiting for transfers between devices  105 us (27%)
  matrix products  92.2 us (24%)
  blocking collectives  84 us (22%)
  local copies, waits for them, and re-layouts  52 us (14%)
  starting transfers between devices  20.5 us (5%)
  between operations  17.9 us (5%)
  other arithmetic  5.4 us (1%)
    all_gather x1, blocking collectives, body(): gathered = lax.all_gather(own_slots, ('grp', 'col'), axis=0, tiled=True)  46.8 us
    psum x1, blocking collectives, body(): loss_total = lax.psum(local_loss, ('grp', 'col'))  37.2 us
    ppermute x3, waiting for transfers between devices, body(): total_grad = total_grad + lax.ppermute(total_grad, 'grp', swap)  35.2 us
    unnamed x2, waiting for transfers between devices  21.6 us
    dot_general x1, matrix products, body(): jnp.einsum('tij,tic->tjc', adj_tiles, picked_grad, preferred_element_type...  19 us
    dot_general x1, matrix products, body(): jnp.einsum('tij,tjc->tic', adj_tiles, picked, preferred_element_type=jnp....  18.3 us
    dot_general x1, matrix products, body(): jnp.einsum('rt,tic->ric', row_places, products, precision=lax.Precision.H...  16.9 us
    dot_general x1, matrix products, body(): jnp.einsum('rt,tjc->rjc', col_places, back_products, precision=lax.Precis...  16.4 us
  transfers between devices with their start and end apart: 8, of which 8 were waited for; matrix products, arithmetic and copies ran while one was open for 2% of the time, Pallas kernels for 0%

profile of v1, /device:TPU:0, one launch (start us, length us, event | category | flops | bytes accessed | tf_op | source)
XLA Modules:
  0.0 376.8 jit_solution(17138335157911418881)
XLA Ops:
  8.2 46.8 %all-gather = bf16[2528,2,64]{2,1,0:T(2,128)(2,1)S(1)} all-gather(bf16[79,2,64]{2,1,0:T(2,128)(2,1)S(1)} %copy.83), channel_id=2, replica_groups=mesh['grp'=8,'col'=4] {'grp','col'}, dimensions={0}, use_global_device_ids=true | all-gather | bytes 667392 | tf_op jit(solution)/shard_map/all_gather | solution.py:57
  58.3 4.1 %scatter_custom_fusion = s32[418]{0:T(512)S(1)} fusion(s32[632]{0:T(1024)S(1)} %fusion.29, s32[632]{0:T(1024)S(1)} %iota.23, s32[]{:T(128)} %constant.21.clone.1), kind=kCustom, calls=%fused_computation.77 | custom fusion | bytes 1676 | tf_op jit(solution)/shard_map/scatter | solution.py:65
  62.4 2.7 gather_fusion
  66.7 2.5 multiply_convert_fusion.1
  69.2 4.0 %all-to-all-start = ((bf16[2048,4,64]{0,2,1:T(8,128)(2,1)}), bf16[2048,4,64]{0,2,1:T(8,128)(2,1)S(1)}, u32[]{:S(2)}, u32[]{:S(2)}) async-start(bf16[2048,4,64]{0,2,1:T(8,128)(2,1)} %bitcast.8), calls=%async_computation | async-start | bytes 2097152 | tf_op jit(solution)/shard_map/all_to_all | solution.py:78
  74.0 13.6 %all-to-all-done = bf16[2048,4,64]{0,2,1:T(8,128)(2,1)S(1)} async-done(((bf16[2048,4,64]{0,2,1:T(8,128)(2,1)}), bf16[2048,4,64]{0,2,1:T(8,128)(2,1)S(1)}, u32[]{:S(2)}, u32[]{:S(2)}) %all-to-all-start) | async-done | bytes 1048608 | tf_op jit(solution)/shard_map/all_to_all | solution.py:78
  91.8 8.0 %gather_fusion.1 = bf16[192,256,64]{1,2,0:T(8,128)(2,1)} fusion(bf16[32,256,64]{1,2,0:T(8,128)(2,1)S(1)} %copy.87, s32[1024]{0:T(1024)S(1)} %pad_clamp_fusion.2), kind=kCustom, calls=%fused_computation.1 | custom fusion | bytes 12583680 | tf_op jit(solution)/shard_map/gather | solution.py:87
  99.8 18.3 %convolution_bitcast_fusion.1 = f32[192,256,64]{1,2,0:T(8,128)} fusion(bf16[192,256,64]{1,2,0:T(8,128)(2,1)} %gather_fusion.1, bf16[192,256,256]{2,1,0:T(8,128)(2,1)} %param.12), kind=kOutput, calls=%fused_computation.10 | convolution fusion | flops 1610612736 | bytes 44040192 | tf_op jit(solution)/shard_map/tij,tjc->tic/dot_general | solution.py:88
  118.1 16.9 %fusion.2 = f32[32,256,64]{1,0,2:T(8,128)} fusion(f32[192,256,64]{1,2,0:T(8,128)} %convolution_bitcast_fusion.1, s32[192]{0:T(256)S(1)} %bitcast.95, pred[192]{0:T(512)(128)(4,1)S(1)} %iota_compare_fusion.3), kind=kOutput, calls=%fused_computation.7 | convolution fusion | flops 1207971840 | bytes 14681024 | tf_op jit(solution)/shard_map/rt,tic->ric/dot_general | solution.py:89
  135.0 2.2 reshape.175
  137.3 2.1 fusion.12
  139.4 3.6 all-to-all-start.1
  143.2 3.1 fusion.40
  146.3 11.1 %all-to-all-done.1 = bf16[4,2048,64]{1,2,0:T(8,128)(2,1)S(1)} async-done(((bf16[4,2048,64]{1,2,0:T(8,128)(2,1)}), bf16[4,2048,64]{1,2,0:T(8,128)(2,1)S(1)}, u32[]{:S(2)}, u32[]{:S(2)}) %all-to-all-start.1) | async-done | bytes 1048608 | tf_op jit(solution)/shard_map/all_to_all | solution.py:94
  157.4 3.7 multiply_convert_fusion
  163.2 37.2 %all-reduce = (f32[]{:T(128)}, f32[]{:T(128)}) all-reduce(f32[]{:T(128)} %get-tuple-element.28, f32[]{:T(128)} %get-tuple-element.27), channel_id=1, replica_groups=mesh['grp'=8,'col'=4] {'grp','col'}, use_global_device_ids=true, to_apply=%region_5.6 | all-reduce | flops 2 | bytes 16 | tf_op jit(solution)/shard_map/psum | solution.py:153
  200.5 3.4 fusion.39
  205.3 3.5 all-to-all-start.2
  208.9 14.4 %all-to-all-done.2 = bf16[2048,4,64]{0,2,1:T(8,128)(2,1)S(1)} async-done(((bf16[2048,4,64]{0,2,1:T(8,128)(2,1)}), bf16[2048,4,64]{0,2,1:T(8,128)(2,1)S(1)}, u32[]{:S(2)}, u32[]{:S(2)}) %all-to-all-start.2) | async-done | bytes 1048608 | tf_op jit(solution)/shard_map/all_to_all | solution.py:120
  225.1 2.6 reshape.176
  229.5 8.0 %gather_fusion.2 = bf16[192,256,64]{1,2,0:T(8,128)(2,1)} fusion(bf16[32,256,64]{1,2,0:T(8,128)(2,1)S(1)} %copy.95, s32[1024]{0:T(1024)S(1)} %pad_clamp_fusion.1), kind=kCustom, calls=%fused_computation.2 | custom fusion | bytes 12583680 | tf_op jit(solution)/shard_map/gather | solution.py:121
  237.5 19.0 %convolution_bitcast_fusion = f32[192,256,64]{1,2,0:T(8,128)} fusion(bf16[192,256,64]{1,2,0:T(8,128)(2,1)} %gather_fusion.2, bf16[192,256,256]{2,1,0:T(8,128)(2,1)} %param.12), kind=kOutput, calls=%fused_computation.9 | convolution fusion | flops 1610612736 | bytes 44040192 | tf_op jit(solution)/shard_map/tij,tic->tjc/dot_general | solution.py:122
  256.5 16.4 %fusion.13 = bf16[32,256,64]{1,0,2:T(8,128)(2,1)} fusion(f32[192,256,64]{1,2,0:T(8,128)} %convolution_bitcast_fusion, s32[192]{0:T(256)S(1)} %bitcast.94, pred[192]{0:T(512)(128)(4,1)S(1)} %iota_compare_fusion.3), kind=kOutput, calls=%fused_computation.30 | convolution fusion | flops 1208496128 | bytes 13632448 | tf_op jit(solution)/shard_map/rt,tjc->rjc/dot_general | solution.py:128
  272.9 1.9 convert_element_type.80
  276.3 3.5 all-to-all-start.3
  280.2 3.2 convolution_convert_fusion.3
  285.5 8.7 %all-to-all-done.3 = bf16[4,2048,64]{1,2,0:T(8,128)(2,1)S(1)} async-done(((bf16[4,2048,64]{1,2,0:T(8,128)(2,1)}), bf16[4,2048,64]{1,2,0:T(8,128)(2,1)S(1)}, u32[]{:S(2)}, u32[]{:S(2)}) %all-to-all-start.3) | async-done | bytes 1048608 | tf_op jit(solution)/shard_map/all_to_all | solution.py:131
  299.2 21.6 %reduce-scatter.4.cloned.1.call-done = bf16[64,834]{1,0:T(8,128)(2,1)} async-done(((bf16[256,834]{1,0:T(8,128)(2,1)}), bf16[64,834]{1,0:T(8,128)(2,1)}) %reduce-scatter.4.cloned.1.call-update) | async-done | bytes 106768
  323.4 10.0 %collective-permute-done = f32[834,64]{1,0:T(8,128)S(1)} collective-permute-done((f32[834,64]{1,0:T(8,128)S(1)}, f32[834,64]{1,0:T(8,128)S(1)}, u32[]{:S(2)}, u32[]{:S(2)}) %collective-permute-start) | collective-permute-done | bytes 213536 | tf_op jit(solution)/shard_map/ppermute | solution.py:165
  335.0 9.1 %collective-permute-done.1 = f32[834,64]{1,0:T(8,128)S(1)} collective-permute-done((f32[834,64]{1,0:T(8,128)S(1)}, f32[834,64]{1,0:T(8,128)S(1)}, u32[]{:S(2)}, u32[]{:S(2)}) %collective-permute-start.1) | collective-permute-done | bytes 213536 | tf_op jit(solution)/shard_map/ppermute | solution.py:165
  344.2 2.5 collective-permute-start.2
  348.1 16.1 %collective-permute-done.2 = f32[834,64]{1,0:T(8,128)S(1)} collective-permute-done((f32[834,64]{1,0:T(8,128)S(1)}, f32[834,64]{1,0:T(8,128)S(1)}, u32[]{:S(2)}, u32[]{:S(2)}) %collective-permute-start.2) | collective-permute-done | bytes 213536 | tf_op jit(solution)/shard_map/ppermute | solution.py:165
  (109 shorter events, 35.0 us)
Async XLA Ops:
  7.2 59.5 %copy-start = (bf16[2048,256]{1,0:T(8,128)(2,1)S(1)}, bf16[2048,256]{1,0:T(8,128)(2,1)}, u32[]{:S(2)}) copy-start(bf16[2048,256]{1,0:T(8,128)(2,1)} %param.11) | copy-start | bytes 3145732
  55.0 3.2 copy-start.15
  65.1 4.1 %copy-start.4 = (bf16[417,2,256]{2,1,0:T(2,128)(2,1)}, bf16[417,2,256]{2,1,0:T(2,128)(2,1)S(1)}, u32[]{:S(2)}) copy-start(bf16[417,2,256]{2,1,0:T(2,128)(2,1)S(1)} %gather_fusion) | copy-start | bytes 1281028
  69.2 4.6 %copy-start.11 = (s32[8192]{0:T(1024)S(1)}, s32[8192]{0:T(1024)}, u32[]{:S(2)}) copy-start(s32[8192]{0:T(1024)} %param.15) | copy-start | bytes 98308
  69.2 4.7 %copy-start.16 = (s32[1,192,2]{1,2,0:T(2,128)S(1)}, s32[1,192,2]{1,2,0:T(2,128)}, u32[]{:S(2)}) copy-start(s32[1,192,2]{1,2,0:T(2,128)} %param.13) | copy-start | bytes 4612
  69.2 18.4 %all-to-all-start = ((bf16[2048,4,64]{0,2,1:T(8,128)(2,1)}), bf16[2048,4,64]{0,2,1:T(8,128)(2,1)S(1)}, u32[]{:S(2)}, u32[]{:S(2)}) async-start(bf16[2048,4,64]{0,2,1:T(8,128)(2,1)} %bitcast.8), calls=%async_computation | async-start | bytes 2097152 | tf_op jit(solution)/shard_map/all_to_all | solution.py:78
  73.9 13.7 %copy-start.8 = (f32[8192]{0:T(1024)}, f32[8192]{0:T(1024)S(1)}, u32[]{:S(2)}) copy-start(f32[8192]{0:T(1024)S(1)} %convert_element_type.72) | copy-start | bytes 98308
  139.4 3.8 %slice-start = ((bf16[417,2,256]{2,1,0:T(2,128)(2,1)}), bf16[32,2,256]{2,1,0:T(2,128)(2,1)S(1)}, s32[]{:S(2)}) async-start(bf16[417,2,256]{2,1,0:T(2,128)(2,1)} %copy-done.4), calls=%async_computation.6 | async-start | bytes 65536 | tf_op jit(solution)/shard_map/slice | solution.py:70
  139.4 3.8 %copy-start.12 = (s32[2048]{0:T(1024)S(1)}, s32[2048]{0:T(1024)}, u32[]{:S(2)}) copy-start(s32[2048]{0:T(1024)} %param.17) | copy-start | bytes 24580
  139.4 18.1 %all-to-all-start.1 = ((bf16[4,2048,64]{1,2,0:T(8,128)(2,1)}), bf16[4,2048,64]{1,2,0:T(8,128)(2,1)S(1)}, u32[]{:S(2)}, u32[]{:S(2)}) async-start(bf16[4,2048,64]{1,2,0:T(8,128)(2,1)} %fusion.12), calls=%async_computation.1 | async-start | bytes 2097152 | tf_op jit(solution)/shard_map/all_to_all | solution.py:94
  143.0 14.4 %copy-start.17 = (f32[1,256]{1,0:T(1,128)S(1)}, f32[1,256]{1,0:T(1,128)}, u32[]{:S(2)}) copy-start(f32[1,256]{1,0:T(1,128)} %get-tuple-element.34) | copy-start | bytes 3076
  157.4 5.0 %copy-start.14 = (s32[2048]{0:T(1024)S(1)}, s32[2048]{0:T(1024)}, u32[]{:S(2)}) copy-start(s32[2048]{0:T(1024)} %param.16) | copy-start | bytes 24580
  161.1 1.0 copy-start.6
  162.4 41.4 %copy-start.5 = (f32[2048,64]{0,1:T(8,128)}, f32[2048,64]{0,1:T(8,128)S(1)}, u32[]{:S(2)}) copy-start(f32[2048,64]{0,1:T(8,128)S(1)} %get-tuple-element.50) | copy-start | bytes 1572868
  200.5 3.4 dynamic-slice-start
  203.9 1.5 copy-start.1
  205.3 18.0 %all-to-all-start.2 = ((bf16[2048,4,64]{0,2,1:T(8,128)(2,1)}), bf16[2048,4,64]{0,2,1:T(8,128)(2,1)S(1)}, u32[]{:S(2)}, u32[]{:S(2)}) async-start(bf16[2048,4,64]{0,2,1:T(8,128)(2,1)} %bitcast.92), calls=%async_computation.2 | async-start | bytes 2097152 | tf_op jit(solution)/shard_map/all_to_all | solution.py:120
  276.3 17.9 %all-to-all-start.3 = ((bf16[4,2048,64]{1,2,0:T(8,128)(2,1)}), bf16[4,2048,64]{1,2,0:T(8,128)(2,1)S(1)}, u32[]{:S(2)}, u32[]{:S(2)}) async-start(bf16[4,2048,64]{1,2,0:T(8,128)(2,1)} %copy.97), calls=%async_computation.3 | async-start | bytes 2097152 | tf_op jit(solution)/shard_map/all_to_all | solution.py:131
  279.8 40.9 %reduce-scatter.4.cloned.1.call-start = ((), (), s32[]{:S(2)}) async-start(), calls=%async_computation.5 | async-start | bytes 573440
  280.1 3.2 copy-start.2
  285.5 9.0 %copy-start.3 = (bf16[2048,256]{0,1:T(8,128)(2,1)S(1)}, bf16[2048,256]{0,1:T(8,128)(2,1)}, u32[]{:S(2)}) copy-start(bf16[2048,256]{0,1:T(8,128)(2,1)} %copy-done.1) | copy-start | bytes 3145732
  294.2 1.6 copy-start.18
  297.0 0.8 copy-start.13
  297.0 1.8 copy-start.7
  297.0 1.9 copy-start.9
  297.0 2.0 copy-start.10
  321.9 11.6 %collective-permute-start = (f32[834,64]{1,0:T(8,128)S(1)}, f32[834,64]{1,0:T(8,128)S(1)}, u32[]{:S(2)}, u32[]{:S(2)}) collective-permute-start(f32[834,64]{1,0:T(8,128)S(1)} %convert_element_type.87), channel_id=1, source_target_pairs={{0,4},{4,0},{8,12},{12,8},{16,20},{20,16},{24,28},{28,24},{1,5},{5... | collective-permute-start | bytes 640520 | tf_op jit(solution)/shard_map/ppermute | solution.py:165
  333.5 10.7 %collective-permute-start.1 = (f32[834,64]{1,0:T(8,128)S(1)}, f32[834,64]{1,0:T(8,128)S(1)}, u32[]{:S(2)}, u32[]{:S(2)}) collective-permute-start(f32[834,64]{1,0:T(8,128)S(1)} %convert_add_fusion), channel_id=1, source_target_pairs={{0,8},{4,12},{8,0},{12,4},{16,24},{20,28},{24,16},{28,20},{1,9},{5... | collective-permute-start | bytes 640520 | tf_op jit(solution)/shard_map/ppermute | solution.py:165
  344.2 20.0 %collective-permute-start.2 = (f32[834,64]{1,0:T(8,128)S(1)}, f32[834,64]{1,0:T(8,128)S(1)}, u32[]{:S(2)}, u32[]{:S(2)}) collective-permute-start(f32[834,64]{1,0:T(8,128)S(1)} %add.172), channel_id=1, source_target_pairs={{0,16},{4,20},{8,24},{12,28},{16,0},{20,4},{24,8},{28,12},{1,17},{... | collective-permute-start | bytes 640520 | tf_op jit(solution)/shard_map/ppermute | solution.py:165
Sparse Core Ops, SparseCore 0:
  298.9 21.7 reduce-scatter.3
